TPU v7x, 32 devices: a whole 2x2x4 slice. The times are simulated.
32 devices in a mesh: ctx: 2 (over x), tp: 4 (over y, core), dp: 4 (over z).
Axes of the slice: x: 2, y: 2, z: 4, core: 2. Of those that a mesh axis runs over, the one named last changes fastest.
Arguments:
- hidden: bfloat16 [4, 1024, 4096], P('dp', 'ctx', 'tp'), may hold values from -6 to 6
- target: bfloat16 [4, 1024, 4096], P('dp', 'ctx', 'tp'), may hold values from -24 to 24
- gain: float32 [4096], replicated, may hold values from 0.5 to 1.5
- w_query: bfloat16 [4096, 2048], P(('ctx', 'dp'), 'tp'), may hold values from -2.15625 to 2.15625
- w_key: bfloat16 [4096, 512], P(('ctx', 'dp'), 'tp'), may hold values from -0.09375 to 0.09375
- value_matrix: bfloat16 [4096, 512], P(('ctx', 'dp'), 'tp'), may hold values from -0.09375 to 0.09375
- w_out: bfloat16 [2048, 4096], P('tp', ('ctx', 'dp')), may hold values from -0.125 to 0.125
- block_order: int32 [4], replicated, may hold values from 0 to 3, each once
Outputs:
- branch: bfloat16 [4, 1024, 4096], P('dp', 'ctx', 'tp')
- loss: float32 [], replicated
Inputs may be any that keep to these rules, and one draw needn't show every extreme that they name: block_order is a permutation of 0 to 3.
All inputs are finite; a program needn't handle non-finite values.
Results may differ from a plain program's by a relative error of at most 0.013.
The roundings to bfloat16 on the way count: a program that leaves them out, or rounds other values in their place, can miss the bound.
Values may be sent and summed in bfloat16 or wider, within the bound.
A program may use at most 128 MiB of HBM per device.

v0:
```python
import jax
import jax.numpy as jnp
from jax import lax
from jax.sharding import PartitionSpec as P

MODEL_WIDTH = 4096
QUERY_HEADS = 16
KEY_VALUE_HEADS = 4
HEAD_SIZE = 128
rope_base = 500000.0


def shifted(value, axis, by):
    peers = lax.axis_size(axis)
    return lax.ppermute(value, axis, [(i, (i + by) % peers) for i in range(peers)])


def positions(order, start, rows, half):
    index = start + lax.iota(jnp.int32, rows)
    block = index // half
    slots = lax.iota(jnp.int32, order.shape[0])
    chosen = jnp.sum(jnp.where(block[:, None] == slots[None, :], order[None, :], 0), axis=1)
    return chosen * half + index % half


def apply_rotary(values, token_places):
    half = values.shape[-1] // 2
    freqs = rope_base ** (-(jnp.arange(half, dtype=jnp.float32) * 2.0) / values.shape[-1])
    angles = token_places.astype(jnp.float32)[:, None] * freqs[None, :]
    cosine = jnp.cos(angles)[:, None, :]
    sine = jnp.sin(angles)[:, None, :]
    first = values[..., :half]
    second = values[..., half:]
    return jnp.concatenate(
        [first * cosine - second * sine, second * cosine + first * sine], axis=-1
    )


def attend(state, query_rows, qpos, piece, kpos):
    peak, total, accum = state
    rows = piece.shape[1]
    local_heads = query_rows.shape[1]
    pair = piece.reshape(2, rows, local_heads, HEAD_SIZE)
    scores = jnp.einsum(
        "qcgd,kcd->cgqk", query_rows, pair[0], preferred_element_type=jnp.float32
    ) * (1.0 / HEAD_SIZE**0.5)
    allowed = (qpos[:, None] >= kpos[None, :])[None, None]
    scores = jnp.where(allowed, scores, -1e30)
    new_peak = jnp.maximum(peak, jnp.max(scores, axis=-1))
    weights = jnp.where(allowed, jnp.exp(scores - new_peak[..., None]), 0.0)
    factor = jnp.exp(peak - new_peak)
    total = total * factor + jnp.sum(weights, axis=-1)
    update = jnp.einsum(
        "cgqk,kcd->qcgd", weights.astype(jnp.bfloat16), pair[1], preferred_element_type=jnp.float32
    )
    accum = accum * jnp.transpose(factor, (2, 0, 1))[..., None] + update
    return (new_peak, total, accum)


def on_device(hidden, target, gain, w_query, w_key, value_matrix, w_out, block_order):
    rows = hidden.shape[1]
    half = rows // 2
    local = hidden[0]
    whole = lax.all_gather(local, "tp", axis=1, tiled=True)
    wide = whole.astype(jnp.float32)
    normed = (
        wide * lax.rsqrt(jnp.mean(wide * wide, axis=1, keepdims=True) + 1e-05) * gain[None, :]
    ).astype(jnp.bfloat16)
    pieces = (
        lax.all_gather(w_query, ("ctx", "dp"), axis=0, tiled=True),
        lax.all_gather(w_key, ("ctx", "dp"), axis=0, tiled=True),
        lax.all_gather(value_matrix, ("ctx", "dp"), axis=0, tiled=True),
    )
    query_rows, key, value_rows = tuple(
        (jnp.dot(normed, piece, preferred_element_type=jnp.float32) for piece in pieces)
    )
    shard = lax.axis_index("ctx")
    qpos = positions(block_order, shard * rows, rows, half)
    local_heads = w_key.shape[1] // HEAD_SIZE
    query_group = QUERY_HEADS // KEY_VALUE_HEADS
    query_rows = (
        apply_rotary(query_rows.reshape(rows, local_heads * query_group, HEAD_SIZE), qpos)
        .astype(jnp.bfloat16)
        .reshape(rows, local_heads, query_group, HEAD_SIZE)
    )
    key = (
        apply_rotary(key.reshape(rows, local_heads, HEAD_SIZE), qpos)
        .astype(jnp.bfloat16)
        .reshape(rows, local_heads * HEAD_SIZE)
    )
    pair = jnp.stack([key, value_rows.astype(jnp.bfloat16)])
    state = (
        jnp.full((local_heads, query_group, rows), -1e30, jnp.float32),
        jnp.zeros((local_heads, query_group, rows), jnp.float32),
        jnp.zeros((rows, local_heads, query_group, HEAD_SIZE), jnp.float32),
    )
    count = lax.axis_size("ctx")
    state = attend(state, query_rows, qpos, pair, qpos)

    def turn(step, carry):
        moved, inner = carry
        moved = shifted(moved, "ctx", 1)
        source = (shard - step) % count
        return (
            moved,
            attend(
                inner, query_rows, qpos, moved, positions(block_order, source * rows, rows, half)
            ),
        )

    moved_end, state = lax.fori_loop(1, count, turn, (pair, state))
    peak, total, accum = state
    attn = (
        (accum / jnp.transpose(total, (2, 0, 1))[..., None])
        .astype(jnp.bfloat16)
        .reshape(rows, local_heads * query_group * HEAD_SIZE)
    )
    terms = jnp.dot(
        attn,
        lax.all_gather(w_out, ("ctx", "dp"), axis=1, tiled=True),
        preferred_element_type=jnp.float32,
    )
    summed = lax.psum_scatter(terms.astype(jnp.bfloat16), "tp", scatter_dimension=1, tiled=True)
    resid = local.astype(jnp.float32) + summed.astype(jnp.float32) - target[0].astype(jnp.float32)
    squares = lax.psum(jnp.sum(resid * resid), ("ctx", "tp", "dp"))
    loss = squares / (lax.axis_size("dp") * lax.axis_size("ctx") * rows * MODEL_WIDTH)
    return (summed[None], loss)


def solution(mesh):
    in_specs = (
        P("dp", "ctx", "tp"),
        P("dp", "ctx", "tp"),
        P(),
        P(("ctx", "dp"), "tp"),
        P(("ctx", "dp"), "tp"),
        P(("ctx", "dp"), "tp"),
        P("tp", ("ctx", "dp")),
        P(),
    )
    out_specs = (P("dp", "ctx", "tp"), P())
    return jax.shard_map(
        on_device, mesh=mesh, in_specs=in_specs, out_specs=out_specs, check_vma=False
    )
```

profile of v0, /device:TPU:0, one launch (start us, length us, event | category | flops | bytes accessed | tf_op | source)
XLA Modules:
  0.0 378.8 jit_solution(6131819200116777629)
XLA Ops:
  7.2 0.7 all-gather.15.cloned.1.call-update
  8.0 0.7 all-gather.7.cloned.1.call-update
  8.7 0.7 all-gather.11.cloned.1.call-update
  9.4 0.5 all-gather.9.cloned.1.call-update
  10.0 0.5 all-gather.13.cloned.1.call-update
  10.7 0.7 select_reduce_fusion
  11.4 1.8 multiply_cosine_fusion
  13.2 0.4 broadcast_compare_fusion
  13.6 33.2 %all-gather.15.cloned.1.call-done = bf16[1,512,4096]{2,1,0:T(8,128)(2,1)} async-done(((bf16[1,512,1024]{2,1,0:T(8,128)(2,1)}), bf16[1,512,4096]{2,1,0:T(8,128)(2,1)}) %all-gather.15.cloned.1.call-update) | async-done | bytes 4194320 | tf_op jit(solution)/shard_map/all_gather | solution.py:64
  46.8 3.1 fusion
  49.9 39.3 %all-gather.7.cloned.1.call-done = bf16[4096,128]{1,0:T(8,128)(2,1)} async-done(((bf16[512,128]{1,0:T(8,128)(2,1)}), bf16[4096,128]{1,0:T(8,128)(2,1)}) %all-gather.7.cloned.1.call-update) | async-done | bytes 1048592 | tf_op jit(solution)/shard_map/all_gather | solution.py:71
  89.2 4.1 %convolution_bitcast_fusion = f32[512,1,128]{0,2,1:T(8,128)S(1)} fusion(bf16[4096,128]{1,0:T(8,128)(2,1)} %all-gather.7.cloned.1.call-done, bf16[1,512,4096]{2,1,0:T(8,128)(2,1)} %all-gather.15.cloned.1.call-done, f32[4096]{0:T(1024)S(1)} %copy-done.4, f32[512]{0:T(512)S(1)} %add_rsqrt_fusion), kind=kOutput, calls=%fused_computation.31 | convolution fusion | flops 545259520 | bytes 5523456 | tf_op jit(solution)/shard_map/dot_general | solution.py:75
  93.3 0.6 fusion.41
  93.9 36.5 %all-gather.11.cloned.1.call-done = bf16[4096,128]{1,0:T(8,128)(2,1)} async-done(((bf16[512,128]{1,0:T(8,128)(2,1)}), bf16[4096,128]{1,0:T(8,128)(2,1)}) %all-gather.11.cloned.1.call-update) | async-done | bytes 1048592 | tf_op jit(solution)/shard_map/all_gather | solution.py:72
  130.4 4.1 %convolution_convert_fusion.1 = bf16[512,128]{0,1:T(8,128)(2,1)S(1)} fusion(bf16[4096,128]{1,0:T(8,128)(2,1)} %all-gather.11.cloned.1.call-done, bf16[1,512,4096]{2,1,0:T(8,128)(2,1)} %all-gather.15.cloned.1.call-done, f32[4096]{0:T(1024)S(1)} %copy-done.4, f32[512]{0:T(512)S(1)} %add_rsqrt_fusion), kind=kOutput, calls=%fused_computation.32 | convolution fusion | flops 545325056 | bytes 5392384 | tf_op jit(solution)/shard_map/dot_general | solution.py:75
  134.5 0.8 pad_maximum_fusion.1
  135.3 0.6 collective-permute-start
  135.9 68.1 %all-gather.9.cloned.1.call-done = bf16[4096,512]{1,0:T(8,128)(2,1)} async-done(((bf16[512,512]{1,0:T(8,128)(2,1)}), bf16[4096,512]{1,0:T(8,128)(2,1)}) %all-gather.9.cloned.1.call-update) | async-done | bytes 4194320 | tf_op jit(solution)/shard_map/all_gather | solution.py:70
  203.9 5.9 %fusion.74 = f32[512,512]{0,1:T(8,128)S(1)} fusion(bf16[4096,512]{1,0:T(8,128)(2,1)} %all-gather.9.cloned.1.call-done, bf16[1,512,4096]{2,1,0:T(8,128)(2,1)} %all-gather.15.cloned.1.call-done, f32[4096]{0:T(1024)S(1)} %copy-done.4, f32[512]{0:T(512)S(1)} %add_rsqrt_fusion), kind=kOutput, calls=%fused_computation.109 | convolution fusion | flops 2155872256 | bytes 9455616 | tf_op jit(solution)/shard_map/dot_general | solution.py:75
  210.3 0.3 copy.32
  210.6 1.2 subtract_convert_fusion
  211.9 1.2 fusion.3
  213.1 2.1 fusion.4
  215.3 1.0 fusion.5
  216.3 1.2 fusion.7
  217.6 1.3 fusion.28
  218.9 2.2 divide_convert_fusion
  221.1 57.8 %all-gather.13.cloned.1.call-done = bf16[512,4096]{1,0:T(8,128)(2,1)} async-done(((bf16[512,512]{1,0:T(8,128)(2,1)}), bf16[512,4096]{1,0:T(8,128)(2,1)}) %all-gather.13.cloned.1.call-update) | async-done | bytes 4194320 | tf_op jit(solution)/shard_map/all_gather | solution.py:120
  279.0 6.5 %convolution_convert_fusion = bf16[512,4096]{1,0:T(8,128)(2,1)} fusion(bf16[512,512]{0,1:T(8,128)(2,1)S(1)} %bitcast.172, bf16[512,4096]{1,0:T(8,128)(2,1)} %all-gather.13.cloned.1.call-done), kind=kOutput, calls=%fused_computation.5 | convolution fusion | flops 2149580800 | bytes 8912896 | tf_op jit(solution)/shard_map/dot_general | solution.py:118
  285.6 42.7 %reduce-scatter.2.cloned.1.call-done = bf16[512,1024]{1,0:T(8,128)(2,1)} async-done(((bf16[512,4096]{1,0:T(8,128)(2,1)}), bf16[512,1024]{1,0:T(8,128)(2,1)}) %reduce-scatter.2.cloned.1.call-update) | async-done | bytes 1048592 | tf_op jit(solution)/shard_map/reduce_scatter | solution.py:123
  328.3 2.4 fusion.12
  330.7 39.5 %psum.7 = f32[]{:T(128)} all-reduce(f32[]{:T(128)} %fusion.12), channel_id=1, replica_groups=mesh['ctx'=2,'tp'=4,'dp'=4] {'ctx','tp','dp'}, use_global_device_ids=true, to_apply=%region_9.10 | all-reduce | flops 1 | bytes 8 | tf_op jit(solution)/shard_map/psum | solution.py:125
  (27 shorter events, 0.8 us)
Async XLA Ops:
  7.2 82.0 %copy-start.4 = (f32[4096]{0:T(1024)S(1)}, f32[4096]{0:T(1024)}, u32[]{:S(2)}) copy-start(f32[4096]{0:T(1024)} %param.10) | copy-start | bytes 49156
  7.2 39.6 %all-gather.15.cloned.1.call-start = ((), (), s32[]{:S(2)}) async-start(), calls=%async_computation.6 | async-start | bytes 5242880 | tf_op jit(solution)/shard_map/all_gather | solution.py:64
  7.9 81.3 %all-gather.7.cloned.1.call-start = ((), (), s32[]{:S(2)}) async-start(), calls=%async_computation.1 | async-start | bytes 1179648 | tf_op jit(solution)/shard_map/all_gather | solution.py:71
  8.7 121.8 %all-gather.11.cloned.1.call-start = ((), (), s32[]{:S(2)}) async-start(), calls=%async_computation.3 | async-start | bytes 1179648 | tf_op jit(solution)/shard_map/all_gather | solution.py:72
  9.4 194.5 %all-gather.9.cloned.1.call-start = ((), (), s32[]{:S(2)}) async-start(), calls=%async_computation.2 | async-start | bytes 4718592 | tf_op jit(solution)/shard_map/all_gather | solution.py:70
  10.0 269.0 %all-gather.13.cloned.1.call-start = ((), (), s32[]{:S(2)}) async-start(), calls=%async_computation.4 | async-start | bytes 4718592 | tf_op jit(solution)/shard_map/all_gather | solution.py:120
  10.6 317.7 %reduce-scatter.2.cloned.1.call-start = ((), (), s32[]{:S(2)}) async-start(), calls=%async_computation.5 | async-start | bytes 5242880 | tf_op jit(solution)/shard_map/reduce_scatter | solution.py:123
  134.5 1.4 copy-start.2
  135.3 77.8 %collective-permute-start = (bf16[2,512,128]{1,2,0:T(8,128)(2,1)}, bf16[2,512,128]{1,2,0:T(8,128)(2,1)}, u32[]{:S(2)}, u32[]{:S(2)}) collective-permute-start(bf16[2,512,128]{1,2,0:T(8,128)(2,1)} %pad_maximum_fusion.1), channel_id=1, source_target_pairs={{0,16},{16,0},{1,17},{17,1},{2,18},{18,2},{3,19},{19,3},{4,20},{20... | collective-permute-start | bytes 786440 | tf_op jit(solution)/shard_map/while/body/eval_jaxpr/ppermute | solution.py:15
  215.2 2.3 copy-start.3
  285.5 42.8 %copy-start = (bf16[1,512,1024]{2,1,0:T(8,128)(2,1)S(1)}, bf16[1,512,1024]{2,1,0:T(8,128)(2,1)}, u32[]{:S(2)}) copy-start(bf16[1,512,1024]{2,1,0:T(8,128)(2,1)} %param.8) | copy-start | bytes 3145732
  285.5 42.8 %copy-start.1 = (bf16[1,512,1024]{2,1,0:T(8,128)(2,1)S(1)}, bf16[1,512,1024]{2,1,0:T(8,128)(2,1)}, u32[]{:S(2)}) copy-start(bf16[1,512,1024]{2,1,0:T(8,128)(2,1)} %param.9) | copy-start | bytes 3145732
Sparse Core Ops, SparseCore 0:
  9.5 37.1 all-gather.14
  48.9 40.2 all-gather.6
  91.3 39.0 all-gather.10
  132.4 71.5 all-gather.8
  205.8 73.1 all-gather.12
  285.7 42.5 reduce-scatter.1
where the time goes:
time: 379 us
  waiting for transfers between devices  281 us (74%)
  blocking collectives  39.5 us (10%)
  matrix products  27.6 us (7%)
  between operations  16.1 us (4%)
  other arithmetic  13.3 us (4%)
    all_gather x1, waiting for transfers between devices, on_device(): lax.all_gather(w_query, ('ctx', 'dp'), axis=0, tiled=True)  68.1 us
    all_gather x1, waiting for transfers between devices, on_device(): lax.all_gather(w_out, ('ctx', 'dp'), axis=1, tiled=True)  57.8 us
    reduce_scatter x1, waiting for transfers between devices, on_device(): lax.psum_scatter(terms.astype(jnp.bfloat16), 'tp', scatter_dimension=1, t...  42.7 us
    psum x1, blocking collectives, on_device(): squares = lax.psum(jnp.sum(resid * resid), ('ctx', 'tp', 'dp'))  39.5 us
    all_gather x1, waiting for transfers between devices, on_device(): lax.all_gather(w_key, ('ctx', 'dp'), axis=0, tiled=True)  39.3 us
    all_gather x1, waiting for transfers between devices, on_device(): lax.all_gather(value_matrix, ('ctx', 'dp'), axis=0, tiled=True)  36.5 us
    all_gather x1, waiting for transfers between devices, on_device(): whole = lax.all_gather(local, 'tp', axis=1, tiled=True)  33.2 us
    dot_general x3, matrix products, on_device(): jnp.dot(normed, piece, preferred_element_type=jnp.float32)  14.1 us
  transfers between devices with their start and end apart: 7, of which 6 were waited for; matrix products, arithmetic and copies ran while one was open for 9% of the time, Pallas kernels for 0%

commit v1 on v0

--- a/solution.py
+++ b/solution.py
@@ -69,7 +69,12 @@
     pieces = (
         lax.all_gather(w_query, ("ctx", "dp"), axis=0, tiled=True),
         lax.all_gather(w_key, ("ctx", "dp"), axis=0, tiled=True),
-        lax.all_gather(value_matrix, ("ctx", "dp"), axis=0, tiled=True),
+        jnp.concatenate(
+            lax.all_to_all(
+                jnp.stack([value_matrix] * lax.axis_size(("ctx", "dp"))), ("ctx", "dp"), 0, 0
+            ),
+            axis=0,
+        ),
     )
     query_rows, key, value_rows = tuple(
         (jnp.dot(normed, piece, preferred_element_type=jnp.float32) for piece in pieces)

time: 379 us -> 339 us (0.89)
  waiting for transfers between devices: 281 us -> 232 us
  starting transfers between devices: 0.82 us -> 8.19 us
    all_gather x1 -> x0, waiting for transfers between devices: 36.5 us -> none  [on_device(): lax.all_gather(value_matrix, ('ctx', 'dp'), axis=0, tiled=True)]
    all_gather x1, waiting for transfers between devices: 33.2 us -> 25 us  [on_device(): whole = lax.all_gather(local, 'tp', axis=1, tiled=True)]
    all_to_all x0 -> x1, starting transfers between devices: none -> 7.41 us  [on_device(): lax.all_to_all(jnp.stack([value_matrix] * lax.axis_size(('ctx', 'dp'))),...]
  transfers between devices with their start and end apart: 7 -> 7, of which waited for: 6 -> 5; matrix products, arithmetic and copies ran while one was open for 9% -> 10% of each run, Pallas kernels for 0% -> 0%
where the time goes in v1:
time: 339 us; the launch traced here: 338 us
  waiting for transfers between devices  232 us (68%)
  blocking collectives  39.5 us (12%)
  matrix products  27.2 us (8%)
  between operations  15.8 us (5%)
  other arithmetic  12.6 us (4%)
  starting transfers between devices  8.19 us (2%)
    all_gather x1, waiting for transfers between devices, on_device(): lax.all_gather(w_query, ('ctx', 'dp'), axis=0, tiled=True)  64.8 us
    all_gather x1, waiting for transfers between devices, on_device(): lax.all_gather(w_out, ('ctx', 'dp'), axis=1, tiled=True)  57.9 us
    reduce_scatter x1, waiting for transfers between devices, on_device(): lax.psum_scatter(terms.astype(jnp.bfloat16), 'tp', scatter_dimension=1, t...  42.7 us
    psum x1, blocking collectives, on_device(): squares = lax.psum(jnp.sum(resid * resid), ('ctx', 'tp', 'dp'))  39.5 us
    all_gather x1, waiting for transfers between devices, on_device(): lax.all_gather(w_key, ('ctx', 'dp'), axis=0, tiled=True)  39.3 us
    all_gather x1, waiting for transfers between devices, on_device(): whole = lax.all_gather(local, 'tp', axis=1, tiled=True)  25 us
    dot_general x3, matrix products, on_device(): jnp.dot(normed, piece, preferred_element_type=jnp.float32)  13.8 us
    all_to_all x1, starting transfers between devices, on_device(): lax.all_to_all(jnp.stack([value_matrix] * lax.axis_size(('ctx', 'dp'))),...  7.41 us
  transfers between devices with their start and end apart: 7, of which 5 were waited for; matrix products, arithmetic and copies ran while one was open for 10% of the time, Pallas kernels for 0%

profile of v1, /device:TPU:0, one launch (start us, length us, event | category | flops | bytes accessed | tf_op | source)
XLA Modules:
  0.0 338.3 jit_solution(3174210367991846716)
XLA Ops:
  7.2 0.7 all-gather.12.cloned.1.call-update
  8.0 0.7 all-gather.6.cloned.1.call-update
  8.7 0.7 all-gather.8.cloned.1.call-update
  9.4 2.0 stack.6
  11.4 7.4 %all-to-all-start = ((bf16[8,512,128]{2,1,0:T(8,128)(2,1)}), bf16[8,512,128]{2,1,0:T(8,128)(2,1)S(1)}, u32[]{:S(2)}, u32[]{:S(2)}) async-start(bf16[8,512,128]{2,1,0:T(8,128)(2,1)} %stack.6), calls=%async_computation | async-start | bytes 2097152 | tf_op jit(solution)/shard_map/all_to_all | solution.py:73
  18.9 0.5 all-gather.10.cloned.1.call-update
  19.6 1.8 multiply_cosine_fusion
  21.4 0.4 broadcast_compare_fusion
  21.8 25.0 %all-gather.12.cloned.1.call-done = bf16[1,512,4096]{2,1,0:T(8,128)(2,1)} async-done(((bf16[1,512,1024]{2,1,0:T(8,128)(2,1)}), bf16[1,512,4096]{2,1,0:T(8,128)(2,1)}) %all-gather.12.cloned.1.call-update) | async-done | bytes 4194320 | tf_op jit(solution)/shard_map/all_gather | solution.py:64
  46.8 3.1 fusion
  49.9 39.3 %all-gather.6.cloned.1.call-done = bf16[4096,128]{1,0:T(8,128)(2,1)} async-done(((bf16[512,128]{1,0:T(8,128)(2,1)}), bf16[4096,128]{1,0:T(8,128)(2,1)}) %all-gather.6.cloned.1.call-update) | async-done | bytes 1048592 | tf_op jit(solution)/shard_map/all_gather | solution.py:71
  89.2 4.1 %convolution_bitcast_fusion = f32[512,1,128]{0,2,1:T(8,128)S(1)} fusion(bf16[4096,128]{1,0:T(8,128)(2,1)} %all-gather.6.cloned.1.call-done, bf16[1,512,4096]{2,1,0:T(8,128)(2,1)} %all-gather.12.cloned.1.call-done, f32[4096]{0:T(1024)S(1)} %copy-done.5, f32[512]{0:T(512)S(1)} %add_rsqrt_fusion), kind=kOutput, calls=%fused_computation.31 | convolution fusion | flops 545259520 | bytes 5523456 | tf_op jit(solution)/shard_map/dot_general | solution.py:80
  93.3 0.6 fusion.41
  93.9 3.8 %convolution_convert_fusion.1 = bf16[512,128]{0,1:T(8,128)(2,1)S(1)} fusion(bf16[4096,128]{1,0:T(8,128)(2,1)S(1)} %bitcast.167, bf16[1,512,4096]{2,1,0:T(8,128)(2,1)} %all-gather.12.cloned.1.call-done, f32[4096]{0:T(1024)S(1)} %copy-done.5, f32[512]{0:T(512)S(1)} %add_rsqrt_fusion), kind=kOutput, calls=%fused_computation.32 | convolution fusion | flops 545325056 | bytes 5392384 | tf_op jit(solution)/shard_map/dot_general | solution.py:80
  97.7 0.7 pad_maximum_fusion.1
  98.4 0.6 collective-permute-start
  99.0 64.8 %all-gather.8.cloned.1.call-done = bf16[4096,512]{1,0:T(8,128)(2,1)} async-done(((bf16[512,512]{1,0:T(8,128)(2,1)}), bf16[4096,512]{1,0:T(8,128)(2,1)}) %all-gather.8.cloned.1.call-update) | async-done | bytes 4194320 | tf_op jit(solution)/shard_map/all_gather | solution.py:70
  163.8 5.9 %fusion.74 = f32[512,512]{0,1:T(8,128)S(1)} fusion(bf16[4096,512]{1,0:T(8,128)(2,1)} %all-gather.8.cloned.1.call-done, bf16[1,512,4096]{2,1,0:T(8,128)(2,1)} %all-gather.12.cloned.1.call-done, f32[4096]{0:T(1024)S(1)} %copy-done.5, f32[512]{0:T(512)S(1)} %add_rsqrt_fusion), kind=kOutput, calls=%fused_computation.109 | convolution fusion | flops 2155872256 | bytes 9455616 | tf_op jit(solution)/shard_map/dot_general | solution.py:80
  169.8 0.3 copy.31
  170.1 0.3 copy.32
  170.5 1.2 subtract_convert_fusion
  171.7 1.2 fusion.3
  173.0 2.1 fusion.4
  175.1 1.0 fusion.5
  176.1 1.2 fusion.7
  177.4 1.3 fusion.28
  178.8 2.2 divide_convert_fusion
  181.0 57.9 %all-gather.10.cloned.1.call-done = bf16[512,4096]{1,0:T(8,128)(2,1)} async-done(((bf16[512,512]{1,0:T(8,128)(2,1)}), bf16[512,4096]{1,0:T(8,128)(2,1)}) %all-gather.10.cloned.1.call-update) | async-done | bytes 4194320 | tf_op jit(solution)/shard_map/all_gather | solution.py:125
  238.8 6.5 %convolution_convert_fusion = bf16[512,4096]{1,0:T(8,128)(2,1)} fusion(bf16[512,512]{0,1:T(8,128)(2,1)S(1)} %bitcast.174, bf16[512,4096]{1,0:T(8,128)(2,1)} %all-gather.10.cloned.1.call-done), kind=kOutput, calls=%fused_computation.5 | convolution fusion | flops 2149580800 | bytes 8912896 | tf_op jit(solution)/shard_map/dot_general | solution.py:123
  245.4 42.7 %reduce-scatter.2.cloned.1.call-done = bf16[512,1024]{1,0:T(8,128)(2,1)} async-done(((bf16[512,4096]{1,0:T(8,128)(2,1)}), bf16[512,1024]{1,0:T(8,128)(2,1)}) %reduce-scatter.2.cloned.1.call-update) | async-done | bytes 1048592 | tf_op jit(solution)/shard_map/reduce_scatter | solution.py:128
  288.1 2.4 fusion.12
  290.5 39.5 %psum.7 = f32[]{:T(128)} all-reduce(f32[]{:T(128)} %fusion.12), channel_id=1, replica_groups=mesh['ctx'=2,'tp'=4,'dp'=4] {'ctx','tp','dp'}, use_global_device_ids=true, to_apply=%region_9.10 | all-reduce | flops 1 | bytes 8 | tf_op jit(solution)/shard_map/psum | solution.py:130
  (29 shorter events, 0.5 us)
Async XLA Ops:
  7.2 12.3 %copy-start.4 = (s32[4]{0:T(128)S(1)}, s32[4]{0:T(128)}, u32[]{:S(2)}) copy-start(s32[4]{0:T(128)} %param.15) | copy-start | bytes 52
  7.2 39.6 %all-gather.12.cloned.1.call-start = ((), (), s32[]{:S(2)}) async-start(), calls=%async_computation.6 | async-start | bytes 5242880 | tf_op jit(solution)/shard_map/all_gather | solution.py:64
  7.9 81.3 %all-gather.6.cloned.1.call-start = ((), (), s32[]{:S(2)}) async-start(), calls=%async_computation.2 | async-start | bytes 1179648 | tf_op jit(solution)/shard_map/all_gather | solution.py:71
  8.7 155.1 %all-gather.8.cloned.1.call-start = ((), (), s32[]{:S(2)}) async-start(), calls=%async_computation.3 | async-start | bytes 4718592 | tf_op jit(solution)/shard_map/all_gather | solution.py:70
  11.4 77.8 %copy-start.5 = (f32[4096]{0:T(1024)S(1)}, f32[4096]{0:T(1024)}, u32[]{:S(2)}) copy-start(f32[4096]{0:T(1024)} %param.10) | copy-start | bytes 49156
  11.4 82.5 %all-to-all-start = ((bf16[8,512,128]{2,1,0:T(8,128)(2,1)}), bf16[8,512,128]{2,1,0:T(8,128)(2,1)S(1)}, u32[]{:S(2)}, u32[]{:S(2)}) async-start(bf16[8,512,128]{2,1,0:T(8,128)(2,1)} %stack.6), calls=%async_computation | async-start | bytes 2097152 | tf_op jit(solution)/shard_map/all_to_all | solution.py:73
  18.8 220.0 %all-gather.10.cloned.1.call-start = ((), (), s32[]{:S(2)}) async-start(), calls=%async_computation.4 | async-start | bytes 4718592 | tf_op jit(solution)/shard_map/all_gather | solution.py:125
  19.4 268.8 %reduce-scatter.2.cloned.1.call-start = ((), (), s32[]{:S(2)}) async-start(), calls=%async_computation.5 | async-start | bytes 5242880 | tf_op jit(solution)/shard_map/reduce_scatter | solution.py:128
  97.7 72.1 %copy-start.2 = (bf16[512,128]{0,1:T(8,128)(2,1)}, bf16[512,128]{0,1:T(8,128)(2,1)S(1)}, u32[]{:S(2)}) copy-start(bf16[512,128]{0,1:T(8,128)(2,1)S(1)} %convolution_convert_fusion.1) | copy-start | bytes 393220
  98.4 74.5 %collective-permute-start = (bf16[2,512,128]{1,2,0:T(8,128)(2,1)}, bf16[2,512,128]{1,2,0:T(8,128)(2,1)}, u32[]{:S(2)}, u32[]{:S(2)}) collective-permute-start(bf16[2,512,128]{1,2,0:T(8,128)(2,1)} %pad_maximum_fusion.1), channel_id=1, source_target_pairs={{0,16},{16,0},{1,17},{17,1},{2,18},{18,2},{3,19},{19,3},{4,20},{20... | collective-permute-start | bytes 786440 | tf_op jit(solution)/shard_map/while/body/eval_jaxpr/ppermute | solution.py:15
  175.1 2.3 copy-start.3
  245.4 42.8 %copy-start = (bf16[1,512,1024]{2,1,0:T(8,128)(2,1)S(1)}, bf16[1,512,1024]{2,1,0:T(8,128)(2,1)}, u32[]{:S(2)}) copy-start(bf16[1,512,1024]{2,1,0:T(8,128)(2,1)} %param.8) | copy-start | bytes 3145732
  245.4 42.8 %copy-start.1 = (bf16[1,512,1024]{2,1,0:T(8,128)(2,1)S(1)}, bf16[1,512,1024]{2,1,0:T(8,128)(2,1)}, u32[]{:S(2)}) copy-start(bf16[1,512,1024]{2,1,0:T(8,128)(2,1)} %param.9) | copy-start | bytes 3145732
Sparse Core Ops, SparseCore 0:
  9.5 37.1 all-gather.11
  48.9 40.2 all-gather.5
  91.3 72.4 all-gather.7
  165.6 73.1 all-gather.9
  245.5 42.5 reduce-scatter.1
